TPU v7x, 128 devices: a whole 4x4x4 slice. The times are simulated.
128 devices in a mesh: seq: 16 (over y_hi, z, core), tp: 8 (over x, y_lo).
Axes of the slice: x: 4, y: 4 (y_hi: 2, y_lo: 2; y = y_hi * 2 + y_lo), z: 4, core: 2. Of those that a mesh axis runs over, the one named last changes fastest.
Arguments:
- streams: bfloat16 [8192, 4, 4096], P('seq', None, 'tp'), may hold values from -6 to 6
- doc_ids: int32 [8192], P('seq'), may hold values from 0 to 3, never falling along the last dimension, each value on 1 to 4096 neighbouring positions
- mix_weight: float32 [4, 4096, 24], P(None, 'tp'), may hold values from -0.046875 to 0.046875
- mix_bias: float32 [24], replicated, may hold values from -1 to 1
- attn_gain: float32 [4096], replicated, may hold values from 0.1 to 1.9
- w_qkv: bfloat16 [4096, 3, 4096], P(None, None, 'tp'), may hold values from -1 to 1
- w_out: bfloat16 [4096, 4096], P('tp'), may hold values from -0.5 to 0.5
Outputs:
- new_streams: bfloat16 [8192, 4, 4096], P('seq', None, 'tp')
Inputs may be any that keep to these rules, and one draw needn't show every extreme that they name: doc_ids never fall along the sequence; each of the 4 documents has 1 to 4096 positions, and the longest has exactly 4096.
All inputs are finite; a program needn't handle non-finite values.
Results may differ from a plain program's by a relative error of at most 0.014.
The roundings to bfloat16 on the way count: a program that leaves them out, or rounds other values in their place, can miss the bound.
Values may be sent and summed in bfloat16 or wider, within the bound.
A program may use at most 256 MiB of HBM per device.

v0:
```python
import jax
import jax.numpy as jnp
from jax import lax
from jax.sharding import Mesh
from jax.sharding import PartitionSpec as P

D = 4096
HEAD_DIM = 128
STREAMS = 4
BALANCE_ROUNDS = 20
TP = ("tp_0", "tp_1")
masked_score = -1e30
norm_eps = 1e-06


def from_everyone(x, axis):
    copies = jnp.broadcast_to(x, (lax.axis_size(axis), *x.shape))
    return lax.all_to_all(copies, axis, split_axis=0, concat_axis=0, tiled=True)


def taken_together(x, axis):
    return from_everyone(x, axis).sum(axis=0)


def packed_total(arrays, axis):
    vector, at, done = (jnp.concatenate([a.reshape(-1) for a in arrays]), 0, [])
    subtotal = taken_together(vector, axis)
    for a in arrays:
        done.append(subtotal[at : at + a.size].reshape(a.shape))
        at += a.size
    return tuple(done)


def gathered_by_axis(x, axes, dim):
    if not axes:
        return x
    nearer = lax.all_gather(x, axes[-1], axis=dim, tiled=True)
    return gathered_by_axis(nearer, axes[:-1], dim)


def summed_rows(terms, axes):
    subtotal = terms.astype(jnp.bfloat16)
    for axis in axes:
        subtotal = lax.psum_scatter(subtotal, axis, scatter_dimension=0, tiled=True)
    return subtotal.astype(jnp.float32)


def doubly_stochastic(mixing_matrix):

    def balance_round(round_index, running_matrix):
        running_matrix = running_matrix / jnp.sum(running_matrix, axis=2, keepdims=True)
        return running_matrix / jnp.sum(running_matrix, axis=1, keepdims=True)

    return lax.fori_loop(0, BALANCE_ROUNDS, balance_round, mixing_matrix)


def coefficients(squares, partial_logits, mix_bias):
    root_mean = jnp.sqrt(squares / (STREAMS * D) + norm_eps)
    coef_logits = partial_logits / root_mean[:, None] + mix_bias
    input_weights = jax.nn.sigmoid(coef_logits[:, :STREAMS])
    output_weights = 2.0 * jax.nn.sigmoid(coef_logits[:, STREAMS : 2 * STREAMS])
    unnormalized_mixing = jnp.exp(coef_logits[:, 2 * STREAMS :]).reshape(-1, STREAMS, STREAMS)
    return (input_weights, output_weights, doubly_stochastic(unnormalized_mixing))


def attend(running, queries, keys_values, key_doc, query_pos, query_doc):
    top_score, denominator, weighted = running
    key_count = keys_values.shape[0]
    heads_local = queries.shape[1]
    keys = keys_values[:, 0].reshape(key_count, heads_local, HEAD_DIM)
    values = keys_values[:, 1].reshape(key_count, heads_local, HEAD_DIM)
    scores = jnp.einsum(
        "qhd,khd->qhk", queries, keys, preferred_element_type=jnp.float32
    ) * HEAD_DIM ** (-0.5)
    key_pos = jnp.arange(key_count, dtype=jnp.int32)
    allowed = ((key_pos[None, :] <= query_pos[:, None]) & (key_doc[None, :] == query_doc[:, None]))[
        :, None, :
    ]
    scores = jnp.where(allowed, scores, masked_score)
    new_top = jnp.maximum(top_score, jnp.max(scores, axis=2))
    weights = jnp.where(allowed, jnp.exp(scores - new_top[:, :, None]), 0.0)
    denominator = jnp.sum(weights, axis=2)
    weighted = jnp.einsum(
        "qhk,khd->qhd", weights.astype(jnp.bfloat16), values, preferred_element_type=jnp.float32
    )
    return (new_top, denominator, weighted)


def local(streams, doc_ids, mix_weight, mix_bias, attn_gain, w_qkv, w_out):
    token_rows = streams.shape[0]
    width_local = streams.shape[2]
    heads_local = width_local // HEAD_DIM
    wide_streams = streams.astype(jnp.float32)
    squares = jnp.sum(wide_streams * wide_streams, axis=(1, 2))
    partial_logits = jnp.einsum(
        "tsd,sdc->tc", wide_streams, mix_weight, precision=lax.Precision.HIGHEST
    )
    squares_all, logits_all = packed_total((squares, partial_logits), TP)
    input_weights, output_weights, mixing = coefficients(squares_all, logits_all, mix_bias)
    mixed_input = jnp.einsum(
        "ts,tsd->td", input_weights, wide_streams, precision=lax.Precision.HIGHEST
    ).astype(jnp.bfloat16)
    flat_weight = w_qkv.reshape(w_qkv.shape[0], 3 * width_local)
    piece_wide = gathered_by_axis(mixed_input, TP, 1).astype(jnp.float32)
    gained = (piece_wide * attn_gain).astype(jnp.bfloat16)
    summed = jnp.dot(gained, flat_weight, preferred_element_type=jnp.float32)
    summed, square_sum = (summed, jnp.sum(piece_wide * piece_wide, axis=1))
    norm_scale = lax.rsqrt(square_sum / D + norm_eps)
    projected = (
        (summed * norm_scale[:, None]).astype(jnp.bfloat16).reshape(token_rows, 3, width_local)
    )
    queries = projected[:, 0].reshape(token_rows, heads_local, HEAD_DIM)
    keys_values = projected[:, 1:3]
    seq_index = lax.axis_index("seq")
    query_pos = seq_index * token_rows + jnp.arange(token_rows, dtype=jnp.int32)
    first_doc = doc_ids[0]
    running = (
        jnp.full((token_rows, heads_local), masked_score, jnp.float32),
        jnp.zeros((token_rows, heads_local), jnp.float32),
        jnp.zeros((token_rows, heads_local, HEAD_DIM), jnp.float32),
    )
    piece_kv = lax.all_gather(keys_values, "seq", axis=0, tiled=True)
    piece_doc = lax.all_gather(doc_ids, "seq", axis=0, tiled=True)
    needed = (jnp.int32(0) < (seq_index + 1) * token_rows) & (piece_doc[-1] >= first_doc)
    running = lax.cond(
        needed,
        lambda running_matrix: attend(
            running_matrix, queries, piece_kv, piece_doc, query_pos, doc_ids
        ),
        lambda running_matrix: running_matrix,
        running,
    )
    top_score, denominator, weighted = running
    context = (
        (weighted / denominator[:, :, None]).astype(jnp.bfloat16).reshape(token_rows, width_local)
    )
    branch_out = summed_rows(
        lax.dot_general(
            w_out, context, (((0,), (1,)), ((), ())), preferred_element_type=jnp.float32
        ),
        TP,
    )
    carried = jnp.einsum("tij,tjd->tid", mixing, wide_streams, precision=lax.Precision.HIGHEST)
    return (carried + output_weights[:, :, None] * branch_out.T[:, None, :]).astype(jnp.bfloat16)


def solution(mesh):
    split = Mesh(mesh.devices.reshape(mesh.shape["seq"], 4, 2), ("seq", "tp_0", "tp_1"))
    in_specs = (
        P("seq", None, TP),
        P("seq"),
        P(None, TP, None),
        P(),
        P(),
        P(None, None, TP),
        P(TP, None),
    )
    out_specs = P("seq", None, TP)
    return jax.shard_map(local, mesh=split, in_specs=in_specs, out_specs=out_specs, check_vma=False)
```

profile of v0, /device:TPU:1, one launch (start us, length us, event | category | flops | bytes accessed | tf_op | source)
XLA Modules:
  0.0 440.1 jit_solution(9482599936923689184)
XLA Ops:
  6.5 3.3 multiply_reduce_fusion
  9.9 3.6 fusion.27
  13.9 13.1 %all_to_all.6 = f32[8,1,12800]{2,1,0:T(1,128)S(1)} all-to-all(f32[8,1,12800]{2,1,0:T(1,128)S(1)} %broadcast_in_dim.37), channel_id=1, replica_groups=mesh['seq'=16,'tp_0'=4,'tp_1'=2] {'tp_0','tp_1'}, dimensions={0} | all-to-all | bytes 819200 | tf_op jit(solution)/shard_map/all_to_all | solution.py:18
  27.6 0.7 divide_add_fusion
  28.5 5.3 %fusion.41 = bf16[512,1,512]{2,1,0:T(2,128)(2,1)S(1)} fusion(f32[512,4,1]{1,2,0:T(1,128)S(1)} %copy.89, bf16[512,4,512]{2,1,0:T(4,128)(2,1)} %param.11), kind=kOutput, calls=%fused_computation.53 | convolution fusion | flops 12582912 | bytes 2629632 | tf_op jit(solution)/shard_map/ts,tsd->td/dot_general | solution.py:100
  33.8 0.9 copy.102
  34.8 25.8 %all-gather.5.cloned.1.call-done = bf16[512,1024]{1,0:T(8,128)(2,1)} async-done(((bf16[512,512]{1,0:T(8,128)(2,1)}), bf16[512,1024]{1,0:T(8,128)(2,1)}) %all-gather.5.cloned.1.call-update) | async-done | bytes 1048592 | tf_op jit(solution)/shard_map/all_gather | solution.py:37
  60.8 17.1 %copy.81 = bf16[4096,3,512]{0,2,1:T(8,128)(2,1)} copy(bf16[4096,3,512]{2,0,1:T(8,128)(2,1)} %param.16) | data formatting | bytes 25165824 | tf_op args[5]
  78.0 33.4 %all-gather.7.cloned.1.call-done = bf16[512,4096]{1,0:T(8,128)(2,1)} async-done(((bf16[512,1024]{1,0:T(8,128)(2,1)}), bf16[512,4096]{1,0:T(8,128)(2,1)}) %all-gather.7.cloned.1.call-update) | async-done | bytes 4194320 | tf_op jit(solution)/shard_map/all_gather | solution.py:37
  111.4 3.1 fusion.14
  114.5 11.0 %fusion.22 = bf16[512,1536]{1,0:T(8,128)(2,1)S(1)} fusion(bf16[4096,1536]{0,1:T(8,128)(2,1)} %bitcast.48, bf16[512,4096]{1,0:T(8,128)(2,1)} %all-gather.7.cloned.1.call-done, f32[4096]{0:T(1024)S(1)} %copy-done.5, f32[512]{0:T(512)S(1)} %add_rsqrt_fusion), kind=kOutput, calls=%fused_computation.28 | convolution fusion | flops 6450315264 | bytes 18368512 | tf_op jit(solution)/shard_map/dot_general | solution.py:106
  125.5 0.7 copy.82
  126.2 1.0 slice.48
  127.3 0.5 slice.39
  127.9 25.4 %all-gather = s32[16,1,512]{2,1,0:T(1,128)S(1)} all-gather(s32[1,1,512]{2,1,0:T(1,128)S(1)} %bitcast.58), channel_id=1, replica_groups=mesh['seq'=16,'tp_0'=4,'tp_1'=2] {'seq'}, dimensions={0}, use_global_device_ids=true | all-gather | bytes 34816 | tf_op jit(solution)/shard_map/all_gather | solution.py:123
  153.3 0.6 slice.46
  155.1 91.7 %all-gather.9.cloned.1.call-done = bf16[8192,2,512]{0,2,1:T(8,128)(2,1)} async-done(((bf16[512,2,512]{0,2,1:T(8,128)(2,1)}), bf16[8192,2,512]{0,2,1:T(8,128)(2,1)}) %all-gather.9.cloned.1.call-update) | async-done | bytes 16777232 | tf_op jit(solution)/shard_map/all_gather | solution.py:122
  246.8 103.6 %conditional.1 = (f32[512,4]{0,1:T(4,128)S(1)}, f32[512,4,128]{0,2,1:T(8,128)S(1)}) conditional(s32[]{:T(128)} %convert_element_type.35, () %tuple.18, (s32[]{:T(128)}, s32[512]{0:T(512)S(1)}, s32[8192]{0:T(1024)S(1)}, s32[512]{0:T(512)S(1)}, bf16[8192,2,512]{0,2,1:T(8,128)(2,1)}, /*index=5*/bf16[512,3,512]{0,2,1:T(8,128)(2,1)S(1)}) %tuple.51), branch_computations={%region_7.0_spmd, %region_8.11_spmd} | conditional | flops 8820619264 | bytes 290021440 | solution.py:125
  246.8 4.4 %fusion.6 = pred[512,8192]{0,1:T(8,128)(4,1)S(1)} fusion(s32[512]{0:T(512)S(1)} %get-tuple-element.37, s32[512]{0:T(512)S(1)} %broadcast_add_fusion, s32[8192]{0:T(1024)S(1)} %get-tuple-element.36), kind=kLoop, calls=%fused_computation.10 | loop fusion | flops 12582912 | bytes 4231168 | tf_op jit(solution)/shard_map/cond/branch_1_fun/and | solution.py:76
  251.2 13.1 %fusion.40 = (bf16[8192,1,512]{0,2,1:T(8,128)(2,1)}, bf16[8192,1,512]{0,2,1:T(8,128)(2,1)}) fusion(bf16[8192,2,512]{0,2,1:T(8,128)(2,1)} %get-tuple-element.38), kind=kLoop, calls=%fused_computation.52 | loop fusion | bytes 33554432 | tf_op jit(solution)/shard_map/cond/branch_1_fun/slice | solution.py:71
  264.4 27.6 %fusion = (f32[512,4]{0,1:T(4,128)S(1)}, f32[4,8192,512]{2,1,0:T(8,128)}) fusion(pred[512,8192]{0,1:T(8,128)(4,1)S(1)} %fusion.6, bf16[8192,4,128]{0,2,1:T(8,128)(2,1)} %bitcast.50, bf16[512,4,128]{0,2,1:T(8,128)(2,1)S(1)} %bitcast.55), kind=kOutput, calls=%fused_computation.4 | convolution fusion | flops 4345296896 | bytes 80224256 | tf_op jit(solution)/shard_map/cond/branch_1_fun/qhd,khd->qhk/dot_general | solution.py:72
  292.0 35.2 %fusion.7 = f32[512,4,128]{2,0,1:T(8,128)S(1)} fusion(bf16[8192,4,128]{0,2,1:T(8,128)(2,1)} %bitcast.49, f32[4,8192,512]{2,1,0:T(8,128)} %get-tuple-element.56, f32[512,4]{0,1:T(4,128)S(1)} %broadcast_maximum_fusion, pred[512,8192]{0,1:T(8,128)(4,1)} %copy-done.2), kind=kOutput, calls=%fused_computation.11 | convolution fusion | flops 4378853376 | bytes 80748544 | tf_op jit(solution)/shard_map/cond/branch_1_fun/qhk,khd->qhd/dot_general | solution.py:83
  327.2 0.3 copy.93
  327.5 22.9 %fusion.2 = f32[512,4]{0,1:T(4,128)S(1)} fusion(f32[4,8192,512]{2,1,0:T(8,128)} %get-tuple-element.56, f32[512,4]{0,1:T(4,128)S(1)} %broadcast_maximum_fusion, pred[512,8192]{0,1:T(8,128)(4,1)} %copy-done.2), kind=kLoop, calls=%fused_computation.6 | loop fusion | flops 83884032 | bytes 71319552 | tf_op jit(solution)/shard_map/cond/branch_1_fun/reduce_sum | solution.py:82
  350.6 6.6 %fusion.15 = bf16[4096,512]{0,1:T(8,128)(2,1)} fusion(bf16[512,512]{0,1:T(8,128)(2,1)S(1)} %bitcast.53, bf16[512,4096]{1,0:T(8,128)(2,1)} %param.17), kind=kOutput, calls=%fused_computation.22 | convolution fusion | flops 2149580800 | bytes 8912896 | tf_op jit(solution)/shard_map/dot_general | solution.py:138
  357.6 43.2 %reduce-scatter.3.cloned.1.call-done = bf16[1024,512]{0,1:T(8,128)(2,1)} async-done(((bf16[4096,512]{0,1:T(8,128)(2,1)}), bf16[1024,512]{0,1:T(8,128)(2,1)}) %reduce-scatter.3.cloned.1.call-update) | async-done | bytes 1048592 | tf_op jit(solution)/shard_map/reduce_scatter | solution.py:44
  400.7 2.1 while.10
  402.9 0.9 copy.80
  403.7 0.4 copy.79
  404.2 21.3 %reduce-scatter.5.cloned.1.call-done = bf16[512,512]{0,1:T(8,128)(2,1)} async-done(((bf16[1024,512]{0,1:T(8,128)(2,1)}), bf16[512,512]{0,1:T(8,128)(2,1)}) %reduce-scatter.5.cloned.1.call-update) | async-done | bytes 524304 | tf_op jit(solution)/shard_map/reduce_scatter | solution.py:44
  425.5 1.2 convert_bitcast_fusion
  426.7 6.9 %add_convert_fusion = bf16[512,4,512]{2,1,0:T(4,128)(2,1)} fusion(f32[512,4,4]{2,1,0:T(4,128)S(1)} %copy.79, bf16[512,4,512]{2,1,0:T(4,128)(2,1)S(1)} %copy-done.3, f32[512,512]{1,0:T(8,128)S(1)} %convert_bitcast_fusion, f32[512,4]{1,0:T(8,128)} %copy.80), kind=kOutput, calls=%fused_computation.24 | convolution fusion | flops 53477376 | bytes 5283840 | tf_op jit(solution)/shard_map/tij,tjd->tid/dot_general | solution.py:143
  (100 shorter events, 3.7 us)
Async XLA Ops:
  6.5 3.3 copy-start
  6.5 54.0 %all-gather.5.cloned.1.call-start = ((), (), s32[]{:S(2)}) async-start(), calls=%async_computation.3 | async-start | bytes 1572864 | tf_op jit(solution)/shard_map/all_gather | solution.py:37
  34.7 76.7 %all-gather.7.cloned.1.call-start = ((), (), s32[]{:S(2)}) async-start(), calls=%async_computation.4 | async-start | bytes 5242880 | tf_op jit(solution)/shard_map/all_gather | solution.py:37
  60.6 53.9 %copy-start.5 = (f32[4096]{0:T(1024)S(1)}, f32[4096]{0:T(1024)}, u32[]{:S(2)}) copy-start(f32[4096]{0:T(1024)} %param.15) | copy-start | bytes 49156
  60.6 186.2 %all-gather.9.cloned.1.call-start = ((), (), s32[]{:S(2)}) async-start(), calls=%async_computation.5 | async-start | bytes 17825792 | tf_op jit(solution)/shard_map/all_gather | solution.py:122
  114.5 12.8 %copy-start.4 = (s32[512]{0:T(512)S(1)}, s32[512]{0:T(512)}, u32[]{:S(2)}) copy-start(s32[512]{0:T(512)} %param.12) | copy-start | bytes 6148
  127.3 273.4 %reduce-scatter.3.cloned.1.call-start = ((), (), s32[]{:S(2)}) async-start(), calls=%async_computation.6 | async-start | bytes 5242880 | tf_op jit(solution)/shard_map/reduce_scatter | solution.py:44
  251.2 13.2 %copy-start.2 = (pred[512,8192]{0,1:T(8,128)(4,1)}, pred[512,8192]{0,1:T(8,128)(4,1)S(1)}, u32[]{:S(2)}) copy-start(pred[512,8192]{0,1:T(8,128)(4,1)S(1)} %fusion.6) | copy-start | bytes 12582916 | tf_op jit(solution)/shard_map/cond
  350.6 76.1 %copy-start.3 = (bf16[512,4,512]{2,1,0:T(4,128)(2,1)S(1)}, bf16[512,4,512]{2,1,0:T(4,128)(2,1)}, u32[]{:S(2)}) copy-start(bf16[512,4,512]{2,1,0:T(4,128)(2,1)} %param.11) | copy-start | bytes 6291460
  357.2 76.3 %copy-start.1 = (f32[4,512,24]{1,2,0:T(8,128)S(1)}, f32[4,512,24]{1,2,0:T(8,128)}, u32[]{:S(2)}) copy-start(f32[4,512,24]{1,2,0:T(8,128)} %param.13) | copy-start | bytes 589828
  357.2 68.3 %reduce-scatter.5.cloned.1.call-start = ((), (), s32[]{:S(2)}) async-start(), calls=%async_computation.7 | async-start | bytes 1572864 | tf_op jit(solution)/shard_map/reduce_scatter | solution.py:44
Sparse Core Ops, SparseCore 0:
  34.9 25.6 all-gather.4
  62.2 49.1 all-gather.6
  127.4 119.3 all-gather.8
  357.4 43.2 reduce-scatter.2
  402.9 22.5 reduce-scatter.4
where the time goes:
time: 441 us; the launch traced here: 440 us
  waiting for transfers between devices  215 us (49%)
  matrix products  96.2 us (22%)
  blocking collectives  38.5 us (9%)
  other arithmetic  37.8 us (9%)
  local copies, waits for them, and re-layouts  36.6 us (8%)
  between operations  14.6 us (3%)
    all_gather x1, waiting for transfers between devices, local(): piece_kv = lax.all_gather(keys_values, 'seq', axis=0, tiled=True)  91.7 us
    reduce_scatter x2, waiting for transfers between devices, summed_rows(): subtotal = lax.psum_scatter(subtotal, axis, scatter_dimension=0, tiled=True)  64.5 us
    all_gather x2, waiting for transfers between devices, gathered_by_axis(): nearer = lax.all_gather(x, axes[-1], axis=dim, tiled=True)  59.2 us
    dot_general x1, matrix products, attend(): jnp.einsum('qhk,khd->qhd', weights.astype(jnp.bfloat16), values, preferre...  35.2 us
    dot_general x1, matrix products, attend(): jnp.einsum('qhd,khd->qhk', queries, keys, preferred_element_type=jnp.floa...  27.6 us
    all_gather x1, blocking collectives, local(): piece_doc = lax.all_gather(doc_ids, 'seq', axis=0, tiled=True)  25.4 us
    reduce_sum x1, other arithmetic, attend(): denominator = jnp.sum(weights, axis=2)  22.9 us
    unnamed x11, local copies, waits for them, and re-layouts  17.2 us
  transfers between devices with their start and end apart: 5, of which 5 were waited for; matrix products, arithmetic and copies ran while one was open for 5% of the time, Pallas kernels for 0%

commit v1 on v0

--- a/solution.py
+++ b/solution.py
@@ -119,7 +119,10 @@
         jnp.zeros((token_rows, heads_local), jnp.float32),
         jnp.zeros((token_rows, heads_local, HEAD_DIM), jnp.float32),
     )
-    piece_kv = lax.all_gather(keys_values, "seq", axis=0, tiled=True)
+    _load_run = lambda message, along_axis: jnp.concatenate(
+        lax.all_to_all(jnp.stack([message] * lax.axis_size(along_axis)), along_axis, 0, 0), 0
+    )
+    piece_kv = _load_run(keys_values, "seq")
     piece_doc = lax.all_gather(doc_ids, "seq", axis=0, tiled=True)
     needed = (jnp.int32(0) < (seq_index + 1) * token_rows) & (piece_doc[-1] >= first_doc)
     running = lax.cond(

time: 441 us -> 613 us (1.39)
  blocking collectives: 38.5 us -> 287 us
  waiting for transfers between devices: 215 us -> 122 us
  starting transfers between devices: 0.57 us -> 8.38 us
  local copies, waits for them, and re-layouts: 36.6 us -> 44.4 us
    all_gather x1, blocking collectives: 25.4 us -> 274 us  [local(): piece_doc = lax.all_gather(doc_ids, 'seq', axis=0, tiled=True)]
    all_gather x1 -> x0, waiting for transfers between devices: 91.7 us -> none  [local(): piece_kv = lax.all_gather(keys_values, 'seq', axis=0, tiled=True)]
    reshape x0 -> x1, local copies, waits for them, and re-layouts: none -> 9.81 us  [local(): jnp.concatenate(lax.all_to_all(jnp.stack([message] * lax.axis_size(along_...]
    all_to_all x0 -> x1, starting transfers between devices: none -> 7.86 us  [local(): lax.all_to_all(jnp.stack([message] * lax.axis_size(along_axis)), along_ax...]
    slice x1, local copies, waits for them, and re-layouts: 13.1 us -> 6.21 us  [attend(): values = keys_values[:, 1].reshape(key_count, heads_local, HEAD_DIM)]
    unnamed x11 -> x17, local copies, waits for them, and re-layouts: 17.2 us -> 17.1 us
  transfers between devices with their start and end apart: 5 -> 5, of which waited for: 5 -> 4; matrix products, arithmetic and copies ran while one was open for 5% -> 3% of each run, Pallas kernels for 0% -> 0%
where the time goes in v1:
time: 613 us; the launch traced here: 612 us
  blocking collectives  287 us (47%)
  waiting for transfers between devices  122 us (20%)
  matrix products  96.2 us (16%)
  local copies, waits for them, and re-layouts  44.4 us (7%)
  other arithmetic  38.4 us (6%)
  between operations  14.6 us (2%)
  starting transfers between devices  8.38 us (1%)
    all_gather x1, blocking collectives, local(): piece_doc = lax.all_gather(doc_ids, 'seq', axis=0, tiled=True)  274 us
    reduce_scatter x2, waiting for transfers between devices, summed_rows(): subtotal = lax.psum_scatter(subtotal, axis, scatter_dimension=0, tiled=True)  62.7 us
    all_gather x2, waiting for transfers between devices, gathered_by_axis(): nearer = lax.all_gather(x, axes[-1], axis=dim, tiled=True)  59.3 us
    dot_general x1, matrix products, attend(): jnp.einsum('qhk,khd->qhd', weights.astype(jnp.bfloat16), values, preferre...  35.2 us
    dot_general x1, matrix products, attend(): jnp.einsum('qhd,khd->qhk', queries, keys, preferred_element_type=jnp.floa...  27.6 us
    reduce_sum x1, other arithmetic, attend(): denominator = jnp.sum(weights, axis=2)  22.9 us
    unnamed x17, local copies, waits for them, and re-layouts  17.1 us
    all_to_all x1, blocking collectives, from_everyone(): return lax.all_to_all(copies, axis, split_axis=0, concat_axis=0, tiled=True)  13.1 us
  transfers between devices with their start and end apart: 5, of which 4 were waited for; matrix products, arithmetic and copies ran while one was open for 3% of the time, Pallas kernels for 0%

profile of v1, /device:TPU:1, one launch (start us, length us, event | category | flops | bytes accessed | tf_op | source)
XLA Modules:
  0.0 612.1 jit_solution(11458160309153346532)
XLA Ops:
  6.5 3.3 multiply_reduce_fusion
  9.9 3.6 fusion.27
  13.9 13.1 %all_to_all.11 = f32[8,1,12800]{2,1,0:T(1,128)S(1)} all-to-all(f32[8,1,12800]{2,1,0:T(1,128)S(1)} %broadcast_in_dim.37), channel_id=1, replica_groups=mesh['seq'=16,'tp_0'=4,'tp_1'=2] {'tp_0','tp_1'}, dimensions={0} | all-to-all | bytes 819200 | tf_op jit(solution)/shard_map/all_to_all | solution.py:18
  27.6 0.7 divide_add_fusion
  28.3 0.6 fusion.37
  29.1 5.3 fusion.41
  34.4 0.9 copy.107
  35.6 25.6 %all-gather.4.cloned.1.call-done = bf16[512,1024]{1,0:T(8,128)(2,1)} async-done(((bf16[512,512]{1,0:T(8,128)(2,1)}), bf16[512,1024]{1,0:T(8,128)(2,1)}) %all-gather.4.cloned.1.call-update) | async-done | bytes 1048592 | tf_op jit(solution)/shard_map/all_gather | solution.py:37
  61.2 17.1 %copy.84 = bf16[4096,3,512]{0,2,1:T(8,128)(2,1)} copy(bf16[4096,3,512]{2,0,1:T(8,128)(2,1)} %param.16) | data formatting | bytes 25165824 | tf_op args[5]
  78.3 33.7 %all-gather.6.cloned.1.call-done = bf16[512,4096]{1,0:T(8,128)(2,1)} async-done(((bf16[512,1024]{1,0:T(8,128)(2,1)}), bf16[512,4096]{1,0:T(8,128)(2,1)}) %all-gather.6.cloned.1.call-update) | async-done | bytes 4194320 | tf_op jit(solution)/shard_map/all_gather | solution.py:37
  112.0 3.1 fusion.14
  115.1 11.0 %fusion.22 = bf16[512,1536]{1,0:T(8,128)(2,1)S(1)} fusion(bf16[4096,1536]{0,1:T(8,128)(2,1)} %bitcast.51, bf16[512,4096]{1,0:T(8,128)(2,1)} %all-gather.6.cloned.1.call-done, f32[4096]{0:T(1024)S(1)} %copy-done.8, f32[512]{0:T(512)S(1)} %add_rsqrt_fusion), kind=kOutput, calls=%fused_computation.28 | convolution fusion | flops 6450315264 | bytes 18368512 | tf_op jit(solution)/shard_map/dot_general | solution.py:106
  126.1 0.7 copy.85
  126.9 6.0 stack.2
  132.8 7.9 %all-to-all-start.1 = ((bf16[16,512,2,512]{1,3,2,0:T(8,128)(2,1)}), bf16[16,512,2,512]{1,3,2,0:T(8,128)(2,1)}, u32[]{:S(2)}, u32[]{:S(2)}) async-start(bf16[16,512,2,512]{1,3,2,0:T(8,128)(2,1)} %stack.2), calls=%async_computation.1 | async-start | bytes 33554432 | tf_op jit(solution)/shard_map/all_to_all | solution.py:123
  140.7 0.5 slice.39
  141.3 274.4 %all-gather = s32[16,1,512]{2,1,0:T(1,128)S(1)} all-gather(s32[1,1,512]{2,1,0:T(1,128)S(1)} %bitcast.61), channel_id=1, replica_groups=mesh['seq'=16,'tp_0'=4,'tp_1'=2] {'seq'}, dimensions={0}, use_global_device_ids=true | all-gather | bytes 34816 | tf_op jit(solution)/shard_map/all_gather | solution.py:126
  415.7 0.6 slice.48
  417.5 106.6 %conditional.1 = (f32[512,4]{0,1:T(4,128)S(1)}, f32[512,4,128]{0,2,1:T(8,128)S(1)}) conditional(s32[]{:T(128)} %convert_element_type.35, () %tuple.18, (s32[]{:T(128)}, s32[512]{0:T(512)S(1)}, s32[8192]{0:T(1024)S(1)}, s32[512]{0:T(512)S(1)}, bf16[16,512,2,512]{1,3,2,0:T(8,128)(2,1)}, /*index=5*/bf16[512,3,512]{0,2,1:T(8,128)(2,1)S(1)}) %tuple.53), branch_computations={%region_7.0_spmd, %region_8.11_spmd} | conditional | flops 8820619264 | bytes 323575872 | solution.py:128
  417.6 4.4 fusion.6
  422.0 9.8 %copy.101 = bf16[16,2,64,8,512]{4,3,0,2,1:T(8,128)(2,1)S(1)} copy(bf16[16,2,64,8,512]{4,3,2,1,0:T(8,128)(2,1)} %bitcast.16) | data formatting | bytes 33554432 | tf_op jit(solution)/shard_map/reshape | solution.py:122
  431.8 6.2 %fusion.40 = (bf16[8192,1,512]{0,2,1:T(8,128)(2,1)}, bf16[8192,1,512]{0,2,1:T(8,128)(2,1)}) fusion(bf16[8192,2,512]{0,2,1:T(8,128)(2,1)S(1)} %bitcast.50), kind=kLoop, calls=%fused_computation.52 | loop fusion | bytes 33554432 | tf_op jit(solution)/shard_map/cond/branch_1_fun/slice | solution.py:71
  438.1 27.6 %fusion = (f32[512,4]{0,1:T(4,128)S(1)}, f32[4,8192,512]{2,1,0:T(8,128)}) fusion(pred[512,8192]{0,1:T(8,128)(4,1)S(1)} %fusion.6, bf16[8192,4,128]{0,2,1:T(8,128)(2,1)} %bitcast.53, bf16[512,4,128]{0,2,1:T(8,128)(2,1)S(1)} %bitcast.58), kind=kOutput, calls=%fused_computation.4 | convolution fusion | flops 4345296896 | bytes 80224256 | tf_op jit(solution)/shard_map/cond/branch_1_fun/qhd,khd->qhk/dot_general | solution.py:72
  465.7 35.2 %fusion.7 = f32[512,4,128]{2,0,1:T(8,128)S(1)} fusion(bf16[8192,4,128]{0,2,1:T(8,128)(2,1)} %bitcast.52, f32[4,8192,512]{2,1,0:T(8,128)} %get-tuple-element.81, f32[512,4]{0,1:T(4,128)S(1)} %broadcast_maximum_fusion, pred[512,8192]{0,1:T(8,128)(4,1)} %copy-done.2), kind=kOutput, calls=%fused_computation.11 | convolution fusion | flops 4378853376 | bytes 80748544 | tf_op jit(solution)/shard_map/cond/branch_1_fun/qhk,khd->qhd/dot_general | solution.py:83
  501.3 22.9 %fusion.2 = f32[512,4]{0,1:T(4,128)S(1)} fusion(f32[4,8192,512]{2,1,0:T(8,128)} %get-tuple-element.81, f32[512,4]{0,1:T(4,128)S(1)} %broadcast_maximum_fusion, pred[512,8192]{0,1:T(8,128)(4,1)} %copy-done.2), kind=kLoop, calls=%fused_computation.6 | loop fusion | flops 83884032 | bytes 71319552 | tf_op jit(solution)/shard_map/cond/branch_1_fun/reduce_sum | solution.py:82
  524.3 6.6 %fusion.15 = bf16[4096,512]{0,1:T(8,128)(2,1)} fusion(bf16[512,512]{0,1:T(8,128)(2,1)S(1)} %bitcast.56, bf16[512,4096]{1,0:T(8,128)(2,1)} %param.17), kind=kOutput, calls=%fused_computation.22 | convolution fusion | flops 2149580800 | bytes 8912896 | tf_op jit(solution)/shard_map/dot_general | solution.py:141
  531.3 41.4 %reduce-scatter.3.cloned.1.call-done = bf16[1024,512]{0,1:T(8,128)(2,1)} async-done(((bf16[4096,512]{0,1:T(8,128)(2,1)}), bf16[1024,512]{0,1:T(8,128)(2,1)}) %reduce-scatter.3.cloned.1.call-update) | async-done | bytes 1048592 | tf_op jit(solution)/shard_map/reduce_scatter | solution.py:44
  572.7 2.1 while.10
  574.9 0.8 copy.83
  576.2 21.3 %reduce-scatter.5.cloned.1.call-done = bf16[512,512]{0,1:T(8,128)(2,1)} async-done(((bf16[1024,512]{0,1:T(8,128)(2,1)}), bf16[512,512]{0,1:T(8,128)(2,1)}) %reduce-scatter.5.cloned.1.call-update) | async-done | bytes 524304 | tf_op jit(solution)/shard_map/reduce_scatter | solution.py:44
  597.5 1.2 convert_bitcast_fusion
  598.7 6.9 %add_convert_fusion = bf16[512,4,512]{2,1,0:T(4,128)(2,1)} fusion(f32[512,4,4]{2,1,0:T(4,128)S(1)} %copy.82, bf16[512,4,512]{2,1,0:T(4,128)(2,1)S(1)} %copy-done.3, f32[512,512]{1,0:T(8,128)S(1)} %convert_bitcast_fusion, f32[512,4]{1,0:T(8,128)} %copy.83), kind=kOutput, calls=%fused_computation.24 | convolution fusion | flops 53477376 | bytes 5283840 | tf_op jit(solution)/shard_map/tij,tjd->tid/dot_general | solution.py:146
  (107 shorter events, 4.5 us)
Async XLA Ops:
  6.5 3.3 copy-start
  6.5 54.6 %all-gather.4.cloned.1.call-start = ((), (), s32[]{:S(2)}) async-start(), calls=%async_computation.4 | async-start | bytes 1572864 | tf_op jit(solution)/shard_map/all_gather | solution.py:37
  28.3 49.9 %copy-start.4 = (f32[512,24]{0,1:T(8,128)}, f32[512,24]{0,1:T(8,128)S(1)}, u32[]{:S(2)}) copy-start(f32[512,24]{0,1:T(8,128)S(1)} %divide_add_fusion) | copy-start | bytes 147460
  35.3 76.7 %all-gather.6.cloned.1.call-start = ((), (), s32[]{:S(2)}) async-start(), calls=%async_computation.5 | async-start | bytes 5242880 | tf_op jit(solution)/shard_map/all_gather | solution.py:37
  61.2 53.9 %copy-start.8 = (f32[4096]{0:T(1024)S(1)}, f32[4096]{0:T(1024)}, u32[]{:S(2)}) copy-start(f32[4096]{0:T(1024)} %param.15) | copy-start | bytes 49156
  132.8 7.9 %copy-start.7 = (s32[512]{0:T(512)S(1)}, s32[512]{0:T(512)}, u32[]{:S(2)}) copy-start(s32[512]{0:T(512)} %param.12) | copy-start | bytes 6148
  132.8 284.7 %all-to-all-start.1 = ((bf16[16,512,2,512]{1,3,2,0:T(8,128)(2,1)}), bf16[16,512,2,512]{1,3,2,0:T(8,128)(2,1)}, u32[]{:S(2)}, u32[]{:S(2)}) async-start(bf16[16,512,2,512]{1,3,2,0:T(8,128)(2,1)} %stack.2), calls=%async_computation.1 | async-start | bytes 33554432 | tf_op jit(solution)/shard_map/all_to_all | solution.py:123
  140.7 432.0 %reduce-scatter.3.cloned.1.call-start = ((), (), s32[]{:S(2)}) async-start(), calls=%async_computation.6 | async-start | bytes 5242880 | tf_op jit(solution)/shard_map/reduce_scatter | solution.py:44
  422.0 16.1 %copy-start.2 = (pred[512,8192]{0,1:T(8,128)(4,1)}, pred[512,8192]{0,1:T(8,128)(4,1)S(1)}, u32[]{:S(2)}) copy-start(pred[512,8192]{0,1:T(8,128)(4,1)S(1)} %fusion.6) | copy-start | bytes 12582916 | tf_op jit(solution)/shard_map/cond
  524.1 7.1 %copy-start.5 = (f32[512,24]{0,1:T(8,128)S(1)}, f32[512,24]{0,1:T(8,128)}, u32[]{:S(2)}) copy-start(f32[512,24]{0,1:T(8,128)} %copy-done.4) | copy-start | bytes 147460
  524.2 50.7 %copy-start.6 = (f32[512,4]{0,1:T(4,128)S(1)}, f32[512,4]{0,1:T(4,128)}, u32[]{:S(2)}) copy-start(f32[512,4]{0,1:T(4,128)} %get-tuple-element.82) | copy-start | bytes 24580
  524.3 74.4 %copy-start.3 = (bf16[512,4,512]{2,1,0:T(4,128)(2,1)S(1)}, bf16[512,4,512]{2,1,0:T(4,128)(2,1)}, u32[]{:S(2)}) copy-start(bf16[512,4,512]{2,1,0:T(4,128)(2,1)} %param.11) | copy-start | bytes 6291460
  531.0 74.6 %copy-start.1 = (f32[4,512,24]{1,2,0:T(8,128)S(1)}, f32[4,512,24]{1,2,0:T(8,128)}, u32[]{:S(2)}) copy-start(f32[4,512,24]{1,2,0:T(8,128)} %param.13) | copy-start | bytes 589828
  531.0 66.5 %reduce-scatter.5.cloned.1.call-start = ((), (), s32[]{:S(2)}) async-start(), calls=%async_computation.7 | async-start | bytes 1572864 | tf_op jit(solution)/shard_map/reduce_scatter | solution.py:44
Sparse Core Ops, SparseCore 0:
  35.5 25.6 all-gather.3
  62.8 49.1 all-gather.5
  531.1 41.5 reduce-scatter.2
  574.9 22.5 reduce-scatter.4
